TPU v7x, 32 devices: a whole 2x2x4 slice. The times are simulated.
32 devices in a mesh: seq: 8 (over z, core), ch: 4 (over y, x).
Axes of the slice: x: 2, y: 2, z: 4, core: 2. Of those that a mesh axis runs over, the one named last changes fastest.
Arguments:
- input_q: bfloat16 [4096, 8192], P('seq', 'ch'), may hold values from -6 to 6
- input_k: bfloat16 [4096, 8192], P('seq', 'ch'), may hold values from -6 to 6
- input_v: bfloat16 [4096, 8192], P('seq', 'ch'), may hold values from -6 to 6
- grad_out: bfloat16 [4096, 8192], P('seq', 'ch'), may hold values from -6 to 6
- short_filters: float32 [3, 3, 8192], P(None, None, 'ch'), may hold values from -3.5 to 3.5
- long_filter: float32 [128, 8192], P(None, 'ch'), may hold values from -0.5 to 0.5
- skip_gain: float32 [8192], P('ch'), may hold values from 0.5 to 1.5
Outputs:
- grad_input_q: bfloat16 [4096, 8192], P('seq', 'ch')
- grad_input_k: bfloat16 [4096, 8192], P('seq', 'ch')
- grad_input_v: bfloat16 [4096, 8192], P('seq', 'ch')
- grad_long: float32 [128, 8192], P('seq', 'ch')
- grad_short: float32 [3, 3, 8192], P(None, None, 'ch')
- grad_skip: float32 [8192], P('ch')
All inputs are finite; a program needn't handle non-finite values.
Results may differ from a plain program's by a relative error of at most 0.001.
Values may be sent and summed in bfloat16 or wider, within the bound.
A program may use at most 128 MiB of HBM per device.

v0:
```python
import functools

import jax
import jax.numpy as jnp
import numpy as np
from jax import lax
from jax.experimental import pallas as pl
from jax.experimental.pallas import tpu as pltpu
from jax.sharding import PartitionSpec as P

F32 = jnp.float32
BF16 = jnp.bfloat16
ROWS = 16


def transforms(span):
    freq = np.concatenate([np.arange(0, span, 2), np.arange(1, span, 2)]) + 0.5
    angle = np.pi * np.outer(freq, np.arange(span)) / span
    fwd = np.concatenate([np.cos(angle), -np.sin(angle)], 0)
    inv = fwd.T / span

    def halves(mat):
        mat = mat.astype(np.float32)
        high = mat.astype(jnp.bfloat16)
        low = (mat - high.astype(np.float32)).astype(jnp.bfloat16)
        return high, low

    fh, fl = halves(fwd)
    ih, il = halves(inv)
    return (
        np.concatenate([fh, fh, fl], 1),
        np.concatenate([ih, ih, il], 1),
        np.concatenate([np.eye(span)[::-1]] * 2, 1).astype(jnp.bfloat16),
    )


def split(value):
    high = value.astype(BF16)
    low = (value - high.astype(F32)).astype(BF16)
    return high, low


def down(window, by, rows):
    return pltpu.roll(window, by, 0)[8 : 8 + rows]


def up(window, by, rows):
    return pltpu.roll(window, rows + 8 - by, 0)[:rows]


def remote(src, dst, send, recv, target):
    return pltpu.make_async_remote_copy(
        src_ref=src,
        dst_ref=dst,
        send_sem=send,
        recv_sem=recv,
        device_id={"seq": target},
        device_id_type=pl.DeviceIdType.MESH,
    )


def kernel(
    size, length, span, ntap, pad,
    q_ref, k_ref, v_ref, g_ref, q_all, k_all, v_all, g_all,
    sf_ref, lf_ref, gain_ref, fh_ref, ih_ref, flip_ref,
    bq_ref, bk_ref, bv_ref, filt_ref, taps_ref, skip_ref,
    qx, kx, vx, gx, kf, vf, zf, gs, zw, gw, hw, acc, sx, gz, prod, part,
    kp_all, vp_all, qp_all, qn_all, gn_all, kn_all, vn_all,
    mine, theirs, chip, others,
    halo_send, halo_recv, pair_send, pair_recv, chip_send, chip_recv,
):
    width = q_ref.shape[1]
    half = span // 2
    nblk = length // span
    big = span + pad
    tile = pl.program_id(0)
    tiles = kp_all.shape[0]
    chips = size // 2
    block = span // size
    me = lax.axis_index("seq")
    core = lax.rem(me, 2)
    place = me // 2
    partner = me + 1 - 2 * core

    def to_next(t):
        cols = pl.ds(pl.multiple_of(t * width, width), width)
        target = lax.rem(me + 1, size)
        parts = ((k_all, big, kp_all), (v_all, big, vp_all), (q_all, pad, qp_all))
        return [
            remote(src.at[pl.ds(length - rows, rows), cols], dst.at[t], halo_send.at[t, j], halo_recv.at[t, j], target)
            for j, (src, rows, dst) in enumerate(parts)
        ]

    def to_prev(t):
        cols = pl.ds(pl.multiple_of(t * width, width), width)
        target = lax.rem(me + size - 1, size)
        parts = ((q_all, big, qn_all), (g_all, big, gn_all), (k_all, pad, kn_all), (v_all, pad, vn_all))
        return [
            remote(src.at[pl.ds(0, rows), cols], dst.at[t], halo_send.at[t, 3 + j], halo_recv.at[t, 3 + j], target)
            for j, (src, rows, dst) in enumerate(parts)
        ]

    def pair_copy(t):
        return remote(mine.at[t, 1 - core], theirs.at[t], pair_send.at[t], pair_recv.at[t], partner)

    def chip_copy(t, d):
        there = lax.rem(place + d, chips)
        return remote(chip.at[t, there], others.at[t, d], chip_send.at[t, d], chip_recv.at[t, d], there * 2 + core)

    @pl.when(tile == 0)
    def _():
        barrier = pltpu.get_barrier_semaphore()
        for d in range(1, size):
            pl.semaphore_signal(
                barrier, inc=1, device_id={"seq": lax.rem(me + d, size)}, device_id_type=pl.DeviceIdType.MESH
            )
        pl.semaphore_wait(barrier, size - 1)

        def send(t, _):
            @pl.when(me < size - 1)
            def _():
                for copy in to_next(t):
                    copy.start()

            @pl.when(me > 0)
            def _():
                for copy in to_prev(t):
                    copy.start()

            return 0

        lax.fori_loop(0, tiles, send, 0)

        @pl.when(me == 0)
        def _():
            for ref in (kp_all, vp_all, qp_all):
                ref[...] = jnp.zeros_like(ref)

        @pl.when(me == size - 1)
        def _():
            for ref in (qn_all, gn_all, kn_all, vn_all):
                ref[...] = jnp.zeros_like(ref)

    kp_ref, vp_ref, qp_ref = kp_all.at[tile], vp_all.at[tile], qp_all.at[tile]
    qn_ref, gn_ref, kn_ref, vn_ref = qn_all.at[tile], gn_all.at[tile], kn_all.at[tile], vn_all.at[tile]

    def join_chip(t):
        pair_copy(t).wait_recv()
        total = mine[t, core] + theirs[t]
        chip[t] = total
        others[t, 0] = mine[t, core, place] + theirs[t, place]
        for d in range(1, chips):
            chip_copy(t, d).start()

    kx[big : big + length] = k_ref[...].astype(F32)
    vx[big : big + length] = v_ref[...].astype(F32)
    qx[pad : pad + length] = q_ref[...].astype(F32)
    gx[:length] = g_ref[...].astype(F32)

    def taps(which):
        return [jnp.broadcast_to(sf_ref[which, i : i + 1, :], (ROWS, width)) for i in range(ntap)]

    def conv(ref, row, weights):
        window = ref[pl.ds(row - 8, ROWS + 8), :]
        total = weights[0] * window[8:]
        for i in range(1, ntap):
            total = total + weights[i] * down(window, i, ROWS)
        return total

    wk, wv, wq = taps(1), taps(2), taps(0)
    per = span // ROWS

    def make_z(c, _):
        row = pl.multiple_of(c * ROWS, ROWS)
        a = conv(kx, row + pad, wk)
        b = conv(vx, row + pad, wv)
        z = a * b
        kf[pl.ds(row, ROWS), :] = a
        vf[pl.ds(row, ROWS), :] = b
        zf[pl.ds(row, ROWS), :] = z
        return 0

    lax.fori_loop(per + 1, (span + length) // ROWS, make_z, 0, unroll=2)

    def make_g(c, _):
        row = pl.multiple_of(c * ROWS, ROWS)
        gs[pl.ds(row, ROWS), :] = gx[pl.ds(row, ROWS), :] * conv(qx, row + pad, wq)
        return 0

    lax.fori_loop(1, length // ROWS, make_g, 0, unroll=2)

    def forward(block, out):
        high, low = split(block)
        stack = jnp.concatenate([high, low, high], 0)
        out[...] = jnp.dot(fh_ref[...], stack, preferred_element_type=F32)

    def inverse(at, out):
        stack = jnp.concatenate([prod[at, 0], prod[at, 1], prod[at, 0]], 0)
        out[...] = jnp.dot(ih_ref[...], stack, preferred_element_type=F32)

    first = lax.broadcasted_iota(jnp.int32, (span, width), 0) == 0
    forward(lf_ref[...] + jnp.where(first, gain_ref[...], 0.0), hw)

    @pl.when(me > 0)
    def _():
        for copy in to_next(tile):
            copy.wait_recv()

    @pl.when(me < size - 1)
    def _():
        for copy in to_prev(tile):
            copy.wait_recv()

    kx[:big] = kp_ref[...].astype(F32)
    kx[big + length :] = kn_ref[...].astype(F32)
    vx[:big] = vp_ref[...].astype(F32)
    vx[big + length :] = vn_ref[...].astype(F32)
    qx[:pad] = qp_ref[...].astype(F32)
    qx[pad + length :] = qn_ref[...].astype(F32)
    gx[length:] = gn_ref[...].astype(F32)
    lax.fori_loop(0, per + 1, make_z, 0, unroll=2)
    make_z((span + length) // ROWS, 0)
    make_g(0, 0)
    lax.fori_loop(length // ROWS, (length + span + pad) // ROWS, make_g, 0, unroll=2)

    for b in range(nblk + 1):
        forward(zf[b * span : (b + 1) * span, :], zw.at[b])
        forward(gs[b * span : (b + 1) * span, :], gw.at[b])
    acc[...] = jnp.zeros_like(acc)

    @pl.when(tile > 0)
    def _():
        join_chip(tile - 1)

    for b in range(nblk):
        row = b * span
        for c in range(span // ROWS):
            sign = 1 if c * ROWS < half else -1
            re = slice(c * ROWS, (c + 1) * ROWS)
            im = slice(span + c * ROWS, span + (c + 1) * ROWS)
            hr, hi = hw[re], hw[im]
            if sign > 0:
                yr = zw[b + 1, re] - zw[b, im]
                yi = zw[b + 1, im] + zw[b, re]
            else:
                yr = zw[b + 1, re] + zw[b, im]
                yi = zw[b + 1, im] - zw[b, re]
            gr, gi = gw[b, re], gw[b, im]
            ph, plo = split(yr * hr - yi * hi)
            prod[2 * b, 0, re] = ph
            prod[2 * b, 1, re] = plo
            ph, plo = split(yr * hi + yi * hr)
            prod[2 * b, 0, im] = ph
            prod[2 * b, 1, im] = plo
            acc[re] += gr * yr + gi * yi
            acc[im] += gi * yr - gr * yi
        inverse(2 * b, sx.at[pl.ds(row, span)])
        for c in range(span // ROWS):
            sign = 1 if c * ROWS < half else -1
            re = slice(c * ROWS, (c + 1) * ROWS)
            im = slice(span + c * ROWS, span + (c + 1) * ROWS)
            hr, hi = hw[re], hw[im]
            if sign > 0:
                yr = gw[b, re] + gw[b + 1, im]
                yi = gw[b, im] - gw[b + 1, re]
            else:
                yr = gw[b, re] - gw[b + 1, im]
                yi = gw[b, im] + gw[b + 1, re]
            ph, plo = split(yr * hr + yi * hi)
            prod[2 * b + 1, 0, re] = ph
            prod[2 * b + 1, 1, re] = plo
            ph, plo = split(yi * hr - yr * hi)
            prod[2 * b + 1, 0, im] = ph
            prod[2 * b + 1, 1, im] = plo
        inverse(2 * b + 1, gz.at[pl.ds(row, span)])
    for c in range(span // ROWS):
        for start in (0, span):
            rows = slice(start + c * ROWS, start + (c + 1) * ROWS)
            ph, plo = split(acc[rows])
            prod[2 * nblk, 0, rows] = ph
            prod[2 * nblk, 1, rows] = plo
    inverse(2 * nblk, part)

    taps_h = lf_ref[...]
    back_h = jnp.dot(flip_ref[...], jnp.concatenate(split(taps_h), 0), preferred_element_type=F32)
    gain = gain_ref[...]
    line = lax.broadcasted_iota(jnp.int32, (8, width), 0)
    edge_s = jnp.zeros((8, width), F32)
    edge_z = jnp.zeros((8, width), F32)
    for i in range(ntap - 1):
        zrow = zf[length + span + i : length + span + i + 1, :]
        grow = gs[length + i : length + i + 1, :]
        win = zf[length + i + 1 : length + i + 1 + span, :]
        value = jnp.sum(win * back_h, axis=0, keepdims=True) + gain * zrow
        edge_s = jnp.where(line == i, value, edge_s)
        win = gs[length + i : length + i + span, :]
        value = jnp.sum(win * taps_h, axis=0, keepdims=True) + gain * grow
        edge_z = jnp.where(line == i, value, edge_z)
    eq = gx[length : length + 8] * edge_s
    ek = edge_z * vf[length + span : length + span + 8]
    ev = edge_z * kf[length + span : length + span + 8]

    def back(grad, after, weights, out_ref, row, own, sums):
        window = jnp.concatenate([grad, after], 0)
        total = weights[0] * grad
        new = [sums[0] + fold(grad * own)]
        for i in range(1, ntap):
            later = up(window, i, ROWS)
            total = total + weights[i] * later
            new.append(sums[i] + fold(later * own))
        out_ref[pl.ds(row, ROWS), :] = total.astype(BF16)
        return grad[:8], new

    def fold(value):
        total = value[:8]
        for r in range(8, ROWS, 8):
            total = total + value[r : r + 8]
        return total

    steps = length // ROWS

    def last(c, carry):
        after, sums = carry
        row = pl.multiple_of((steps - 1 - c) * ROWS, ROWS)
        gzc = gz[pl.ds(row, ROWS), :]
        gq = gx[pl.ds(row, ROWS), :] * sx[pl.ds(row, ROWS), :]
        gk = gzc * vf[pl.ds(row + span, ROWS), :]
        gv = gzc * kf[pl.ds(row + span, ROWS), :]
        aq, s0 = back(gq, after[0], wq, bq_ref, row, qx[pl.ds(row + pad, ROWS), :], sums[0])
        ak, s1 = back(gk, after[1], wk, bk_ref, row, kx[pl.ds(row + big, ROWS), :], sums[1])
        av, s2 = back(gv, after[2], wv, bv_ref, row, vx[pl.ds(row + big, ROWS), :], sums[2])
        return (aq, ak, av), (s0, s1, s2)

    zero = [jnp.zeros((8, width), F32) for _ in range(ntap)]
    _, sums = lax.fori_loop(0, steps, last, ((eq, ek, ev), (zero, zero, zero)), unroll=2)
    rows = [jnp.sum(sums[w][i], axis=0, keepdims=True) for w in range(3) for i in range(ntap)]
    rows.append(part[0:1, :])
    small = jnp.concatenate(rows + [jnp.zeros((pad - len(rows), width), F32)], 0)
    for d in range(size):
        mine[tile, d % 2, d // 2, :block] = part[d * block : (d + 1) * block]
        mine[tile, d % 2, d // 2, block:] = small
    pair_copy(tile).start()

    @pl.when(tile == tiles - 1)
    def _():
        join_chip(tiles - 1)

        def finish(t, _):
            cols = pl.ds(pl.multiple_of(t * width, width), width)

            @pl.when(me < size - 1)
            def _():
                for copy in to_next(t):
                    copy.wait_send()

            @pl.when(me > 0)
            def _():
                for copy in to_prev(t):
                    copy.wait_send()

            pair_copy(t).wait_send()
            for d in range(1, chips):
                chip_copy(t, d).wait_send()
                chip_copy(t, d).wait_recv()
            total = others[t, place]
            for z in range(1, chips):
                total = total + others[t, lax.rem(place + chips - z, chips)]
            filt_ref[:, cols] = total[:block]
            for w in range(3):
                for i in range(ntap):
                    at = block + w * ntap + i
                    taps_ref[w, i : i + 1, cols] = total[at : at + 1]
            at = block + 3 * ntap
            skip_ref[:, cols] = total[at : at + 1]
            return 0

        lax.fori_loop(0, tiles, finish, 0)


def body(input_q, input_k, input_v, grad_out, short_filters, long_filter, skip_gain):
    length, channels = input_q.shape
    ntap = short_filters.shape[1]
    span = long_filter.shape[0]
    pad = 16
    big = span + pad
    width = min(256, channels)
    mats = [jnp.asarray(m) for m in transforms(span)]
    nblk = length // span

    def tile(rows):
        return pl.BlockSpec((rows, width), lambda i: (0, i))

    def whole(mat):
        return pl.BlockSpec(mat.shape, lambda i: (0, 0))

    size = lax.axis_size("seq")
    tiles = channels // width
    chips = size // 2
    block = span // size
    cells = lambda *rows: pltpu.VMEM((*rows, width), F32)
    edge = lambda rows: pltpu.VMEM((tiles, rows, width), BF16)
    ext = length + big
    full = pl.BlockSpec(memory_space=pl.ANY)
    out = jax.ShapeDtypeStruct((length, channels), BF16)
    back_q, back_k, back_v, grad_filt, grad_taps, grad_gain = pl.pallas_call(
        functools.partial(kernel, size, length, span, ntap, pad),
        grid=(tiles,),
        out_shape=(
            out, out, out,
            jax.ShapeDtypeStruct((block, channels), F32),
            jax.ShapeDtypeStruct((3, ntap, channels), F32),
            jax.ShapeDtypeStruct((1, channels), F32),
        ),
        in_specs=[tile(length)] * 4
        + [full] * 4
        + [pl.BlockSpec((3, ntap, width), lambda i: (0, 0, i)), tile(span), tile(1)]
        + [whole(m) for m in mats],
        out_specs=(
            tile(length), tile(length), tile(length),
            pl.BlockSpec((block, channels), lambda i: (0, 0)),
            pl.BlockSpec((3, ntap, channels), lambda i: (0, 0, 0)),
            pl.BlockSpec((1, channels), lambda i: (0, 0)),
        ),
        scratch_shapes=[
            cells(ext + pad), cells(ext + pad), cells(ext + pad), cells(ext),
            cells(ext), cells(ext), cells(ext), cells(ext),
            cells(nblk + 1, 2 * span), cells(nblk + 1, 2 * span),
            cells(2 * span), cells(2 * span), cells(length), cells(length),
            pltpu.VMEM((2 * nblk + 1, 2, 2 * span, width), BF16), cells(span),
            edge(big), edge(big), edge(pad), edge(big), edge(big), edge(pad), edge(pad),
            cells(tiles, 2, chips, block + pad), cells(tiles, chips, block + pad),
            cells(tiles, chips, block + pad), cells(tiles, chips, block + pad),
            pltpu.SemaphoreType.DMA((tiles, 7)), pltpu.SemaphoreType.DMA((tiles, 7)),
            pltpu.SemaphoreType.DMA((tiles,)), pltpu.SemaphoreType.DMA((tiles,)),
            pltpu.SemaphoreType.DMA((tiles, chips)), pltpu.SemaphoreType.DMA((tiles, chips)),
        ],
        compiler_params=pltpu.CompilerParams(
            dimension_semantics=("arbitrary",),
            vmem_limit_bytes=56 * 1024 * 1024,
            collective_id=0,
            has_side_effects=True,
        ),
        name="hyena_back",
    )(
        input_q, input_k, input_v, grad_out, input_q, input_k, input_v, grad_out,
        short_filters, long_filter, skip_gain[None], *mats,
    )
    return (back_q, back_k, back_v, grad_filt, grad_taps, grad_gain[0])


def solution(mesh):
    return jax.shard_map(
        body,
        mesh=mesh,
        in_specs=(
            P("seq", "ch"),
            P("seq", "ch"),
            P("seq", "ch"),
            P("seq", "ch"),
            P(None, None, "ch"),
            P(None, "ch"),
            P("ch"),
        ),
        out_specs=(
            P("seq", "ch"),
            P("seq", "ch"),
            P("seq", "ch"),
            P("seq", "ch"),
            P(None, None, "ch"),
            P("ch"),
        ),
        check_vma=False,
    )
```

profile of v0, /device:TPU:0, one launch (start us, length us, event | category | flops | bytes accessed | tf_op | source)
XLA Modules:
  0.0 63.8 jit_solution(10449737088222387388)
XLA Ops:
  0.6 54.3 %hyena_back.1 = (bf16[512,2048]{1,0:T(8,128)(2,1)}, bf16[512,2048]{1,0:T(8,128)(2,1)}, bf16[512,2048]{1,0:T(8,128)(2,1)}, f32[16,2048]{1,0:T(8,128)}, f32[3,3,2048]{2,1,0:T(4,128)}, /*index=5*/f32[1,2048]{1,0:T(1,128)}) custom-call(bf16[512,2048]{1,0:T(8,128)(2,1)} %q_all.1, bf16[512,2048]{1,0:T(8,128)(2,1)} %k_all.1, bf16[512,2048]{1,0:T(8,128)(2,1)} %v_all.1, ...), custom_call_target="tpu_custom_call" | custom-call | tf_op jit(solution)/shard_map/hyena_back/pallas_call | solution.py:405
  54.9 0.0 copy-start.1
  54.9 3.3 %copy.22 = bf16[512,2048]{1,0:T(8,128)(2,1)} copy(bf16[512,2048]{1,0:T(8,128)(2,1)} %get-tuple-element.24) | data formatting | bytes 4194304
  58.2 0.0 copy-done.1
  58.2 0.0 copy-start
  58.2 1.3 %copy.23 = bf16[512,2048]{1,0:T(8,128)(2,1)} copy(bf16[512,2048]{1,0:T(8,128)(2,1)S(1)} %copy-done.1) | data formatting | bytes 4194304
  59.6 1.0 %copy-done = bf16[512,2048]{1,0:T(8,128)(2,1)S(1)} copy-done((bf16[512,2048]{1,0:T(8,128)(2,1)S(1)}, bf16[512,2048]{1,0:T(8,128)(2,1)}, u32[]{:S(2)}) %copy-start) | copy-done | bytes 2097176
  60.6 0.0 copy-start.2
  60.6 0.0 copy-start.3
  60.6 0.0 copy-start.4
  60.6 1.3 %copy.24 = bf16[512,2048]{1,0:T(8,128)(2,1)} copy(bf16[512,2048]{1,0:T(8,128)(2,1)S(1)} %copy-done) | data formatting | bytes 4194304
  61.9 0.0 copy-done.2
  61.9 0.7 %copy.25 = f32[16,2048]{1,0:T(8,128)} copy(f32[16,2048]{1,0:T(8,128)S(1)} %copy-done.2) | data formatting | bytes 262144
  62.6 0.0 copy-done.3
  62.6 0.6 %copy.26 = f32[3,3,2048]{2,1,0:T(4,128)} copy(f32[3,3,2048]{2,1,0:T(4,128)S(1)} %copy-done.3) | data formatting | bytes 147456
  63.2 0.0 copy-done.4
  63.2 0.6 copy.27
Async XLA Ops:
  54.9 3.3 %copy-start.1 = (bf16[512,2048]{1,0:T(8,128)(2,1)S(1)}, bf16[512,2048]{1,0:T(8,128)(2,1)}, u32[]{:S(2)}) copy-start(bf16[512,2048]{1,0:T(8,128)(2,1)} %get-tuple-element.25) | copy-start | bytes 6291460
  58.2 2.3 %copy-start = (bf16[512,2048]{1,0:T(8,128)(2,1)S(1)}, bf16[512,2048]{1,0:T(8,128)(2,1)}, u32[]{:S(2)}) copy-start(bf16[512,2048]{1,0:T(8,128)(2,1)} %get-tuple-element.26) | copy-start | bytes 6291460
  60.6 1.3 %copy-start.2 = (f32[16,2048]{1,0:T(8,128)S(1)}, f32[16,2048]{1,0:T(8,128)}, u32[]{:S(2)}) copy-start(f32[16,2048]{1,0:T(8,128)} %get-tuple-element.27) | copy-start | bytes 393220
  60.6 2.0 %copy-start.3 = (f32[3,3,2048]{2,1,0:T(4,128)S(1)}, f32[3,3,2048]{2,1,0:T(4,128)}, u32[]{:S(2)}) copy-start(f32[3,3,2048]{2,1,0:T(4,128)} %get-tuple-element.28) | copy-start | bytes 221188
  60.6 2.6 %copy-start.4 = (f32[1,2048]{1,0:T(1,128)S(1)}, f32[1,2048]{1,0:T(1,128)}, u32[]{:S(2)}) copy-start(f32[1,2048]{1,0:T(1,128)} %get-tuple-element.17) | copy-start | bytes 24580
where the time goes:
time: 64 us; the launch traced here: 63.8 us
  Pallas kernels  54.3 us (85%)
  local copies, waits for them, and re-layouts  8.88 us (14%)
  between operations  0.66 us (1%)
    pallas_call x1, Pallas kernels, body(): pl.pallas_call(functools.partial(kernel, size, length, span, ntap, pad),...  54.3 us
    unnamed x16, local copies, waits for them, and re-layouts  8.88 us

commit v1 on v0

v1 whole, which is shorter than its diff:
```python
import functools

import jax
import jax.numpy as jnp
import numpy as np
from jax import lax
from jax.experimental import pallas as pl
from jax.experimental.pallas import tpu as pltpu
from jax.sharding import PartitionSpec as P

F32 = jnp.float32
BF16 = jnp.bfloat16
ROWS = 16
VMEM_MIB = 52
UNROLL = 2


def transforms(span):
    freq = np.concatenate([np.arange(0, span, 2), np.arange(1, span, 2)]) + 0.5
    angle = np.pi * np.outer(freq, np.arange(span)) / span
    fwd = np.concatenate([np.cos(angle), -np.sin(angle)], 0)
    inv = fwd.T / span

    def halves(mat):
        mat = mat.astype(np.float32)
        high = mat.astype(jnp.bfloat16)
        low = (mat - high.astype(np.float32)).astype(jnp.bfloat16)
        return high, low

    fh, fl = halves(fwd)
    ih, il = halves(inv)
    return (
        np.concatenate([np.concatenate([fh, fh], 1), np.concatenate([fl, fl], 1)], 0),
        np.concatenate([ih, il], 0),
        np.concatenate([np.eye(span)[::-1]] * 2, 1).astype(jnp.bfloat16),
    )


def split(value):
    high = value.astype(BF16)
    low = (value - high.astype(F32)).astype(BF16)
    return high, low


def remote(src, dst, send, recv, target):
    return pltpu.make_async_remote_copy(
        src_ref=src,
        dst_ref=dst,
        send_sem=send,
        recv_sem=recv,
        device_id={"seq": target},
        device_id_type=pl.DeviceIdType.MESH,
    )


def kernel(
    size, length, span, ntap, pad,
    q_all, k_all, v_all, g_all, sf_hbm, lf_hbm, gain_hbm, fh_hbm, ih_hbm, flip_hbm,
    bq_ref, bk_ref, bv_ref, filt_ref, taps_ref, skip_ref,
    q_in, k_in, v_in, g_in, lf_in, sf_ref, gain_in, fh_ref, ih_ref, flip_ref,
    kx, vx, qx, gx, kf, vf, zf, gs, zh, zl, gh, gl, zw, gw, hw, sx, gz, prod, acc, part, gqs, gks, gvs, sums,
    kp_all, vp_all, qp_all, qn_all, gn_all, kn_all, vn_all,
    mine, theirs, chip, others, smine, stheirs, schip, sothers, half, other_half,
    load_sem, fix_sem, halo_send, halo_recv,
    pair_send, pair_recv, chip_send, chip_recv,
    spair_send, spair_recv, schip_send, schip_recv, last_send, last_recv,
):
    _, ncol, _, lane = zh.shape
    width = ncol * lane
    hlf = width // 2
    half_span = span // 2
    nblk = length // span
    big = span + pad
    tile = pl.program_id(0)
    tiles = kp_all.shape[0]
    chips = size // 2
    block = span // size
    me = lax.axis_index("seq")
    core = lax.rem(me, 2)
    place = me // 2
    partner = me + 1 - 2 * core

    def cols_of(t):
        return pl.ds(pl.multiple_of(t * width, width), width)

    def to_next(t):
        cols = cols_of(t)
        target = lax.rem(me + 1, size)
        parts = ((k_all, big, kp_all), (v_all, big, vp_all), (q_all, pad, qp_all))
        return [
            remote(src.at[pl.ds(length - rows, rows), cols], dst.at[t], halo_send.at[t, j], halo_recv.at[t, j], target)
            for j, (src, rows, dst) in enumerate(parts)
        ]

    def to_prev(t):
        cols = cols_of(t)
        target = lax.rem(me + size - 1, size)
        parts = ((q_all, big, qn_all), (g_all, big, gn_all), (k_all, pad, kn_all), (v_all, pad, vn_all))
        return [
            remote(src.at[pl.ds(0, rows), cols], dst.at[t], halo_send.at[t, 3 + j], halo_recv.at[t, 3 + j], target)
            for j, (src, rows, dst) in enumerate(parts)
        ]

    def pair_copy(t):
        return remote(mine.at[t, 1 - core], theirs.at[t], pair_send.at[t], pair_recv.at[t], partner)

    def chip_copy(t, d):
        there = lax.rem(place + d, chips)
        return remote(chip.at[t, there], others.at[t, d], chip_send.at[t, d], chip_recv.at[t, d], there * 2 + core)

    def spair_copy(t):
        return remote(smine.at[t, 1 - core], stheirs.at[t], spair_send.at[t], spair_recv.at[t], partner)

    def schip_copy(t, d):
        there = lax.rem(place + d, chips)
        return remote(schip.at[t], sothers.at[t, d], schip_send.at[t, d], schip_recv.at[t, d], there * 2 + core)

    def last_copy():
        return remote(half, other_half, last_send, last_recv, partner)

    def loads(t):
        cols = cols_of(t)
        pairs = ((k_all, k_in), (v_all, v_in), (q_all, q_in), (g_all, g_in))
        out = [pltpu.make_async_copy(lf_hbm.at[:, cols], lf_in.at[:, cols], load_sem.at[t, 0])]
        for j, (a, b) in enumerate(pairs):
            for c in range(ncol):
                strip = pl.ds(pl.multiple_of(t * width + c * lane, lane), lane)
                out.append(pltpu.make_async_copy(a.at[:, strip], b.at[t * ncol + c], load_sem.at[t, 1 + j * ncol + c]))
        return out

    def fixed():
        pairs = ((sf_hbm, sf_ref), (fh_hbm, fh_ref), (ih_hbm, ih_ref), (flip_hbm, flip_ref), (gain_hbm, gain_in))
        return [pltpu.make_async_copy(a, b, fix_sem.at[j]) for j, (a, b) in enumerate(pairs)]

    @pl.when(tile == 0)
    def _():
        barrier = pltpu.get_barrier_semaphore()
        for d in range(1, size):
            pl.semaphore_signal(
                barrier, inc=1, device_id={"seq": lax.rem(me + d, size)}, device_id_type=pl.DeviceIdType.MESH
            )
        for copy in loads(0) + fixed():
            copy.start()
        pl.semaphore_wait(barrier, size - 1)

        def send(t, _):
            @pl.when(me < size - 1)
            def _():
                for copy in to_next(t):
                    copy.start()

            @pl.when(me > 0)
            def _():
                for copy in to_prev(t):
                    copy.start()

            return 0

        lax.fori_loop(0, tiles, send, 0)

        def fetch(t, _):
            for copy in loads(t):
                copy.start()
            return 0

        lax.fori_loop(1, tiles, fetch, 0)

        @pl.when(me == 0)
        def _():
            for ref in (kp_all, vp_all, qp_all):
                ref[...] = jnp.zeros_like(ref)

        @pl.when(me == size - 1)
        def _():
            for ref in (qn_all, gn_all, kn_all, vn_all):
                ref[...] = jnp.zeros_like(ref)

        for copy in fixed():
            copy.wait()

    kp_ref, vp_ref, qp_ref = kp_all.at[tile], vp_all.at[tile], qp_all.at[tile]
    qn_ref, gn_ref, kn_ref, vn_ref = qn_all.at[tile], gn_all.at[tile], kn_all.at[tile], vn_all.at[tile]

    def join_long(t):
        pair_copy(t).wait_recv()
        chip[t] = mine[t, core] + theirs[t]
        others[t, 0] = mine[t, core, place] + theirs[t, place]
        for d in range(1, chips):
            chip_copy(t, d).start()

    def join_small(t):
        spair_copy(t).wait_recv()
        total = smine[t, core] + stheirs[t]
        schip[t] = total
        sothers[t, 0] = total
        for d in range(1, chips):
            schip_copy(t, d).start()

    for copy in loads(tile):
        copy.wait()

    def here(c):
        return pl.ds(pl.multiple_of(tile * width + c * lane, lane), lane)

    def cut(c):
        return slice(c * lane, (c + 1) * lane)

    def taps(which, c):
        return [jnp.broadcast_to(sf_ref[which, i : i + 1, here(c)], (ROWS, lane)) for i in range(ntap)]

    weights = [[taps(w, c) for c in range(ncol)] for w in range(3)]

    def conv(ref, c, row, first, w):
        total = w[c][0] * first
        for i in range(1, ntap):
            total = total + w[c][i] * ref[c, pl.ds(row - i, ROWS), :]
        return total

    def slot(b):
        return 0 if b == 0 else 3 if b < 0 or b == nblk else 1 + b % 2

    def put(high, low, row, c, value):
        h, l = split(value)
        at = slot(row // span), c, pl.ds(row % span, ROWS)
        high[at] = h
        low[at] = l

    def make_z(row, c, a0, b0, keep_taps, keep_z, keep_split=True):
        a = conv(kx, c, row + big, a0, weights[1])
        b = conv(vx, c, row + big, b0, weights[2])
        z = a * b
        if keep_taps:
            kf[c, pl.ds(row, ROWS), :] = a
            vf[c, pl.ds(row, ROWS), :] = b
        if keep_z:
            zf[c, pl.ds(row - (length - span), ROWS), :] = z
        if keep_split:
            put(zh, zl, row, c, z)

    def make_g(row, c, q0, g0, keep_g, keep_split=True):
        g = g0 * conv(qx, c, row + pad, q0, weights[0])
        if keep_g:
            gs[c, pl.ds(row - length, ROWS), :] = g
        if keep_split:
            put(gh, gl, row, c, g)

    def own(row, c, keep_z):
        a0 = k_in[tile * ncol + c, pl.ds(row, ROWS), :].astype(F32)
        b0 = v_in[tile * ncol + c, pl.ds(row, ROWS), :].astype(F32)
        q0 = q_in[tile * ncol + c, pl.ds(row, ROWS), :].astype(F32)
        g0 = g_in[tile * ncol + c, pl.ds(row, ROWS), :].astype(F32)
        kx[c, pl.ds(row + big, ROWS), :] = a0
        vx[c, pl.ds(row + big, ROWS), :] = b0
        qx[c, pl.ds(row + pad, ROWS), :] = q0
        gx[c, pl.ds(row, ROWS), :] = g0
        make_z(row, c, a0, b0, True, keep_z)
        make_g(row, c, q0, g0, False)

    def wide(strips):
        return jnp.concatenate(list(strips), 1)

    def spectrum(high, low):
        both = jnp.dot(fh_ref[...], jnp.concatenate([high, low], 0), preferred_element_type=F32)
        return both[: 2 * span] + both[2 * span :]

    def forward(high, low, b, out):
        at = slot(b)
        out[...] = spectrum(wide(high[at, c] for c in range(ncol)), wide(low[at, c] for c in range(ncol)))

    gain = gain_in[:, cols_of(tile)]
    taps_h = lf_in[:, cols_of(tile)]
    first = lax.broadcasted_iota(jnp.int32, (span, width), 0) == 0
    hh, hl = split(taps_h + jnp.where(first, gain, 0.0))
    hw[...] = spectrum(hh, hl)
    for c in range(ncol):
        a0 = k_in[tile * ncol + c, :ROWS, :].astype(F32)
        b0 = v_in[tile * ncol + c, :ROWS, :].astype(F32)
        q0 = q_in[tile * ncol + c, :ROWS, :].astype(F32)
        kx[c, big : big + ROWS, :] = a0
        vx[c, big : big + ROWS, :] = b0
        qx[c, pad : pad + ROWS, :] = q0
        gx[c, :ROWS, :] = g_in[tile * ncol + c, :ROWS, :].astype(F32)
    def own_block(b):
        for c in range(ncol):
            for r in range(span // ROWS):
                if b + r > 0:
                    own(b * span + r * ROWS, c, b == nblk - 1)

    early = nblk // 2
    for b in range(early):
        own_block(b)

    @pl.when(me > 0)
    def _():
        for copy in to_next(tile):
            copy.wait_recv()

    @pl.when(me < size - 1)
    def _():
        for copy in to_prev(tile):
            copy.wait_recv()

    for c in range(ncol):
        for ref, src, at in (
            (kx, kp_ref, 0), (vx, vp_ref, 0), (qx, qp_ref, 0),
            (kx, kn_ref, big + length), (vx, vn_ref, big + length), (qx, qn_ref, pad + length),
            (gx, gn_ref, length),
        ):
            ref[c, at : at + src.shape[0], :] = src[:, cut(c)].astype(F32)

    def rows_of(ref, c, row):
        return ref[c, row : row + ROWS, :]

    for c in range(ncol):
        make_z(0, c, rows_of(kx, c, big), rows_of(vx, c, big), True, False)
        make_g(0, c, rows_of(qx, c, pad), rows_of(gx, c, 0), False)
    for b in range(1, early):
        forward(zh, zl, b, zw.at[b + 1])
        forward(gh, gl, b, gw.at[b])
    forward(zh, zl, 0, zw.at[1])
    forward(gh, gl, 0, gw.at[0])
    for b in range(early, nblk):
        own_block(b)
        forward(zh, zl, b, zw.at[b + 1])
        forward(gh, gl, b, gw.at[b])
    for c in range(ncol):
        for r in range(span // ROWS):
            row = r * ROWS - span
            make_z(row, c, rows_of(kx, c, row + big), rows_of(vx, c, row + big), False, False)
    forward(zh, zl, -1, zw.at[0])
    for c in range(ncol):
        for r in range(span // ROWS + 1):
            row = length + r * ROWS
            make_g(row, c, rows_of(qx, c, row + pad), rows_of(gx, c, row), True, r < span // ROWS)
        row = length
        make_z(row, c, rows_of(kx, c, row + big), rows_of(vx, c, row + big), True, True, False)
    forward(gh, gl, nblk, gw.at[nblk])
    back_h = jnp.dot(flip_ref[...], jnp.concatenate(split(taps_h), 0), preferred_element_type=F32)
    line = lax.broadcasted_iota(jnp.int32, (8, lane), 0)
    for c in range(ncol):
        edge_s = jnp.zeros((8, lane), F32)
        edge_z = jnp.zeros((8, lane), F32)
        for i in range(ntap - 1):
            zrow = zf[c, span + i : span + i + 1, :]
            grow = gs[c, i : i + 1, :]
            win = zf[c, i + 1 : i + 1 + span, :]
            value = jnp.sum(win * back_h[:, cut(c)], axis=0, keepdims=True) + gain[:, cut(c)] * zrow
            edge_s = jnp.where(line == i, value, edge_s)
            win = gs[c, i : i + span, :]
            value = jnp.sum(win * taps_h[:, cut(c)], axis=0, keepdims=True) + gain[:, cut(c)] * grow
            edge_z = jnp.where(line == i, value, edge_z)
        gqs[c, length : length + 8, :] = gx[c, length : length + 8, :] * edge_s
        gks[c, length : length + 8, :] = edge_z * vf[c, length : length + 8, :]
        gvs[c, length : length + 8, :] = edge_z * kf[c, length : length + 8, :]

    steps = span // ROWS * ncol

    def product(blocks, sign, n, _):
        if isinstance(n, int):
            re, im = pl.ds(n // ncol * ROWS, ROWS), pl.ds(n // ncol * ROWS + span, ROWS)
            pc = n % ncol
            col = cut(pc)
        else:
            fr = pl.multiple_of(n // ncol * ROWS, ROWS)
            re, im = pl.ds(fr, ROWS), pl.ds(fr + span, ROWS)
            pc = lax.rem(n, ncol)
            col = pl.ds(pl.multiple_of(pc * lane, lane), lane)

        def store(at, rows, value):
            h, l = split(value)
            prod[at, 0, pc, rows, :] = h
            prod[at, 1, pc, rows, :] = l

        hr, hi = hw[re, col], hw[im, col]
        b = blocks[0]
        zr, zi = zw[b, re, col], zw[b, im, col]
        gr, gi = gw[b, re, col], gw[b, im, col]
        ar = ai = None
        if b == 0:
            ar, ai = acc[re, col], acc[im, col]
        for b in blocks:
            zr2, zi2 = zw[b + 1, re, col], zw[b + 1, im, col]
            gr2, gi2 = gw[b + 1, re, col], gw[b + 1, im, col]
            if sign > 0:
                yr, yi = zr2 - zi, zi2 + zr
                xr, xi = gr + gi2, gi - gr2
            else:
                yr, yi = zr2 + zi, zi2 - zr
                xr, xi = gr - gi2, gi + gr2
            store(2 * b, re, yr * hr - yi * hi)
            store(2 * b, im, yr * hi + yi * hr)
            store(2 * b + 1, re, xr * hr + xi * hi)
            store(2 * b + 1, im, xi * hr - xr * hi)
            tr, ti = gr * yr + gi * yi, gi * yr - gr * yi
            ar, ai = (tr, ti) if ar is None else (ar + tr, ai + ti)
            zr, zi, gr, gi = zr2, zi2, gr2, gi2
        if blocks[0] == 0:
            store(2 * nblk, re, ar)
            store(2 * nblk, im, ai)
        else:
            acc[re, col] = ar
            acc[im, col] = ai
        return 0

    @pl.when(tile > 0)
    def _():
        join_long(tile - 1)
        join_small(tile - 1)

    late = range(nblk // 2, nblk)
    lax.fori_loop(0, steps // 2, functools.partial(product, late, 1), 0, unroll=UNROLL)
    lax.fori_loop(steps // 2, steps, functools.partial(product, late, -1), 0, unroll=UNROLL)

    def inverse(at, out):
        both = jnp.dot(ih_ref[...], wide(prod[at, 0, c] for c in range(ncol)), preferred_element_type=F32)
        rest = jnp.dot(ih_ref[:span], wide(prod[at, 1, c] for c in range(ncol)), preferred_element_type=F32)
        out[...] = both[:span] + both[span:] + rest


    def back_to_time(b):
        inverse(2 * b, sx.at[b % 2])
        inverse(2 * b + 1, gz.at[b % 2])

    back_to_time(nblk - 1)
    for n in range(steps):
        product(range(nblk // 2), 1 if n < steps // 2 else -1, n, 0)
    inverse(2 * nblk, part)
    for d in range(size):
        mine[tile, d % 2, d // 2] = part[d * block : (d + 1) * block]
    pair_copy(tile).start()

    def fold(value):
        total = value[:8]
        for r in range(8, ROWS, 8):
            total = total + value[r : r + 8]
        return total

    per = span // ROWS
    sums[...] = jnp.zeros_like(sums)

    def last(b):
        if b > 0:
            back_to_time(b - 1)
        for c in range(ncol):
            total = [[sums[w, i, :, cut(c)] for i in range(ntap)] for w in range(3)]
            for r in range(per):
                row = b * span + (per - 1 - r) * ROWS
                at = pl.ds(row, ROWS)
                inner = slice(row - b * span, row - b * span + ROWS)
                gzc = gz[b % 2, inner, cut(c)]
                grads = (gx[c, at, :] * sx[b % 2, inner, cut(c)], gzc * vf[c, at, :], gzc * kf[c, at, :])
                for w, (grad, ref, own_x, off, out) in enumerate(zip(
                    grads, (gqs, gks, gvs), (qx, kx, vx), (pad, big, big), (bq_ref, bk_ref, bv_ref)
                )):
                    ref[c, at, :] = grad
                    x = own_x[c, pl.ds(row + off, ROWS), :]
                    res = weights[w][c][0] * grad
                    total[w][0] = total[w][0] + fold(grad * x)
                    for i in range(1, ntap):
                        later = ref[c, pl.ds(row + i, ROWS), :]
                        res = res + weights[w][c][i] * later
                        total[w][i] = total[w][i] + fold(later * x)
                    out[tile * ncol + c, at, :] = res.astype(BF16)
            for w in range(3):
                for i in range(ntap):
                    sums[w, i, :, cut(c)] = total[w][i]

    for b in reversed(range(nblk)):
        last(b)
    rows = [jnp.sum(sums[w, i], axis=0, keepdims=True) for w in range(3) for i in range(ntap)]
    rows.append(part[0:1, :])
    small = jnp.concatenate(rows + [jnp.zeros((pad - len(rows), width), F32)], 0)
    for p in range(2):
        smine[tile, p] = small[:, p * hlf : (p + 1) * hlf]
    spair_copy(tile).start()

    @pl.when(tile == tiles - 1)
    def _():
        join_long(tiles - 1)
        join_small(tiles - 1)

        def finish(t, _):
            cols = cols_of(t)

            @pl.when(me < size - 1)
            def _():
                for copy in to_next(t):
                    copy.wait_send()

            @pl.when(me > 0)
            def _():
                for copy in to_prev(t):
                    copy.wait_send()

            pair_copy(t).wait_send()
            spair_copy(t).wait_send()
            for d in range(1, chips):
                chip_copy(t, d).wait_send()
                chip_copy(t, d).wait_recv()
                schip_copy(t, d).wait_send()
                schip_copy(t, d).wait_recv()
            total = others[t, place]
            small = sothers[t, place]
            for z in range(1, chips):
                d = lax.rem(place + chips - z, chips)
                total = total + others[t, d]
                small = small + sothers[t, d]
            filt_ref[:, cols] = total
            half[t] = small
            return 0

        lax.fori_loop(0, tiles, finish, 0)
        last_copy().start()
        last_copy().wait()

        def write(t, _):
            for p in range(2):
                own_half = half[t]
                total = jnp.where(core == p, own_half, other_half[t])
                cols = pl.ds(pl.multiple_of(t * width + p * hlf, hlf), hlf)
                for w in range(3):
                    for i in range(ntap):
                        at = w * ntap + i
                        taps_ref[w, i : i + 1, cols] = total[at : at + 1]
                skip_ref[:, cols] = total[3 * ntap : 3 * ntap + 1]
            return 0

        lax.fori_loop(0, tiles, write, 0)


def settle(*refs):
    half = len(refs) // 2
    sem = refs[-1]
    copies = []
    for src, dst in zip(refs[:half], refs[half:-1]):
        if src.shape == dst.shape:
            copies.append((src, dst))
        else:
            lane = src.shape[2]
            copies += [(src.at[n], dst.at[:, n * lane : (n + 1) * lane]) for n in range(src.shape[0])]
    copies = [pltpu.make_async_copy(src, dst, sem.at[n]) for n, (src, dst) in enumerate(copies)]
    for copy in copies:
        copy.start()
    for copy in copies:
        copy.wait()


def body(input_q, input_k, input_v, grad_out, short_filters, long_filter, skip_gain):
    length, channels = input_q.shape
    ntap = short_filters.shape[1]
    span = long_filter.shape[0]
    pad = 16
    lane = 128
    big = span + pad
    width = min(256, channels)
    mats = [jnp.asarray(m) for m in transforms(span)]
    nblk = length // span

    size = lax.axis_size("seq")
    tiles = channels // width
    chips = size // 2
    block = span // size
    ncol = width // lane
    cells = lambda *rows: pltpu.VMEM((*rows, width), F32)
    strips = lambda rows: pltpu.VMEM((ncol, rows, lane), F32)
    halves = lambda *rows: pltpu.VMEM((*rows, lane), BF16)
    edge = lambda rows: pltpu.VMEM((tiles, rows, width), BF16)
    small = lambda *lead: pltpu.VMEM((*lead, pad, width // 2), F32)
    dma = lambda *shape: pltpu.SemaphoreType.DMA(shape)
    whole = pl.BlockSpec(memory_space=pltpu.VMEM)
    outs = pl.pallas_call(
        functools.partial(kernel, size, length, span, ntap, pad),
        grid=(tiles,),
        out_shape=(
            *[pltpu.VMEM((tiles * ncol, length, lane), BF16) for _ in range(3)],
            pltpu.VMEM((block, channels), F32),
            pltpu.VMEM((3, ntap, channels), F32),
            pltpu.VMEM((1, channels), F32),
        ),
        in_specs=[pl.BlockSpec(memory_space=pltpu.HBM)] * 10,
        out_specs=(whole,) * 6,
        scratch_shapes=[
            *[pltpu.VMEM((tiles * ncol, length, lane), BF16) for _ in range(4)],
            pltpu.VMEM((span, channels), F32), pltpu.VMEM((3, ntap, channels), F32), pltpu.VMEM((1, channels), F32),
            *[pltpu.VMEM(m.shape, BF16) for m in mats],
            strips(length + big + pad), strips(length + big + pad), strips(length + big + pad), strips(length + big),
            strips(length + pad), strips(length + pad), strips(span + pad), strips(span + pad),
            *[halves(4, ncol, span) for _ in range(4)],
            cells(nblk + 1, 2 * span), cells(nblk + 1, 2 * span), cells(2 * span), cells(2, span), cells(2, span),
            halves(2 * nblk + 1, 2, ncol, 2 * span), cells(2 * span), cells(span),
            strips(length + pad), strips(length + pad), strips(length + pad), cells(3, ntap, 8),
            edge(big), edge(big), edge(pad), edge(big), edge(big), edge(pad), edge(pad),
            cells(tiles, 2, chips, block), cells(tiles, chips, block),
            cells(tiles, chips, block), cells(tiles, chips, block),
            small(tiles, 2), small(tiles), small(tiles), small(tiles, chips), small(tiles), small(tiles),
            dma(tiles, 1 + 4 * ncol), dma(5), dma(tiles, 7), dma(tiles, 7),
            dma(tiles), dma(tiles), dma(tiles, chips), dma(tiles, chips),
            dma(tiles), dma(tiles), dma(tiles, chips), dma(tiles, chips),
            pltpu.SemaphoreType.DMA, pltpu.SemaphoreType.DMA,
        ],
        compiler_params=pltpu.CompilerParams(
            dimension_semantics=("arbitrary",),
            vmem_limit_bytes=VMEM_MIB * 1024 * 1024,
            collective_id=0,
            has_side_effects=True,
        ),
        name="hyena_back",
    )(input_q, input_k, input_v, grad_out, short_filters, long_filter, skip_gain[None], *mats)
    outs = [pltpu.with_memory_space_constraint(out, pltpu.VMEM) for out in outs]
    back_q, back_k, back_v, grad_filt, grad_taps, grad_gain = pl.pallas_call(
        settle,
        out_shape=tuple(
            jax.ShapeDtypeStruct((length, channels) if n < 3 else out.shape, out.dtype) for n, out in enumerate(outs)
        ),
        in_specs=[whole] * 6,
        out_specs=(pl.BlockSpec(memory_space=pltpu.HBM),) * 6,
        scratch_shapes=[dma(3 * tiles * ncol + 3)],
        compiler_params=pltpu.CompilerParams(vmem_limit_bytes=1024 * 1024),
        name="settle",
    )(*outs)
    return (back_q, back_k, back_v, grad_filt, grad_taps, grad_gain[0])


def solution(mesh):
    return jax.shard_map(
        body,
        mesh=mesh,
        in_specs=(
            P("seq", "ch"),
            P("seq", "ch"),
            P("seq", "ch"),
            P("seq", "ch"),
            P(None, None, "ch"),
            P(None, "ch"),
            P("ch"),
        ),
        out_specs=(
            P("seq", "ch"),
            P("seq", "ch"),
            P("seq", "ch"),
            P("seq", "ch"),
            P(None, None, "ch"),
            P("ch"),
        ),
        check_vma=False,
    )
```

time: 64 us -> 51.7 us (0.81)
  local copies, waits for them, and re-layouts: 8.88 us -> 0 us
  Pallas kernels: 54.3 us -> 50.9 us
    unnamed x16 -> x0, local copies, waits for them, and re-layouts: 8.88 us -> none
    pallas_call x1, Pallas kernels: 54.3 us -> 47.7 us  [body(): pl.pallas_call(functools.partial(kernel, size, length, span, ntap, pad),...]
    pallas_call x0 -> x1, Pallas kernels: none -> 3.13 us  [body(): pl.pallas_call(settle, out_shape=tuple((jax.ShapeDtypeStruct((length, cha...]
where the time goes in v1:
time: 51.7 us; the launch traced here: 51.5 us
  Pallas kernels  50.9 us (98%)
  between operations  0.64 us (1%)
    pallas_call x1, Pallas kernels, body(): pl.pallas_call(functools.partial(kernel, size, length, span, ntap, pad),...  47.7 us
    pallas_call x1, Pallas kernels, body(): pl.pallas_call(settle, out_shape=tuple((jax.ShapeDtypeStruct((length, cha...  3.13 us

profile of v1, /device:TPU:0, one launch (start us, length us, event | category | flops | bytes accessed | tf_op | source)
XLA Modules:
  0.0 51.5 jit_solution(16382695972362087897)
XLA Ops:
  0.6 47.7 %hyena_back.1 = (bf16[16,512,128]{2,1,0:T(8,128)(2,1)S(1)}, bf16[16,512,128]{2,1,0:T(8,128)(2,1)S(1)}, bf16[16,512,128]{2,1,0:T(8,128)(2,1)S(1)}, f32[16,2048]{1...) custom-call(bf16[512,2048]{1,0:T(8,128)(2,1)} %q_all.1, bf16[512,2048]{1,0:T(8,128)(2,1)} %k_all.1, ...), custom_call_target="tpu_custom_call" | custom-call | tf_op jit(solution)/shard_map/hyena_back/pallas_call | solution.py:571
  48.4 3.1 %settle.1 = (bf16[512,2048]{1,0:T(8,128)(2,1)}, bf16[512,2048]{1,0:T(8,128)(2,1)}, bf16[512,2048]{1,0:T(8,128)(2,1)}, f32[16,2048]{1,0:T(8,128)}, f32[3,3,2048]{2,1,0:T(4,128)}, /*index=5*/f32[1,2048]{1,0:T(1,128)}) custom-call(bf16[16,512,128]{2,1,0:T(8,128)(2,1)S(1)} %get-tuple-element.18.refs_0_, bf16[16,512,128]{2,1,0:T(8,128)(2,1)S(1)} %get-tuple-element.19.refs_1_, ...), custom_call_target="tpu_custom_call" | custom-call | tf_op jit(solution)/shard_map/settle/pallas_call | solution.py:610

commit v2 on v1

--- a/solution.py
+++ b/solution.py
@@ -199,6 +199,21 @@
     for copy in loads(tile):
         copy.wait()
 
+    @pl.when(tile > 1)
+    def _():
+        join_long(tile - 2)
+        join_small(tile - 2)
+
+    @pl.when(me > 0)
+    def _():
+        for copy in to_next(tile):
+            copy.wait_recv()
+
+    @pl.when(me < size - 1)
+    def _():
+        for copy in to_prev(tile):
+            copy.wait_recv()
+
     def here(c):
         return pl.ds(pl.multiple_of(tile * width + c * lane, lane), lane)
 
@@ -217,7 +232,7 @@
         return total
 
     def slot(b):
-        return 0 if b == 0 else 3 if b < 0 or b == nblk else 1 + b % 2
+        return nblk if b < 0 else b
 
     def put(high, low, row, c, value):
         h, l = split(value)
@@ -273,34 +288,6 @@
     hh, hl = split(taps_h + jnp.where(first, gain, 0.0))
     hw[...] = spectrum(hh, hl)
     for c in range(ncol):
-        a0 = k_in[tile * ncol + c, :ROWS, :].astype(F32)
-        b0 = v_in[tile * ncol + c, :ROWS, :].astype(F32)
-        q0 = q_in[tile * ncol + c, :ROWS, :].astype(F32)
-        kx[c, big : big + ROWS, :] = a0
-        vx[c, big : big + ROWS, :] = b0
-        qx[c, pad : pad + ROWS, :] = q0
-        gx[c, :ROWS, :] = g_in[tile * ncol + c, :ROWS, :].astype(F32)
-    def own_block(b):
-        for c in range(ncol):
-            for r in range(span // ROWS):
-                if b + r > 0:
-                    own(b * span + r * ROWS, c, b == nblk - 1)
-
-    early = nblk // 2
-    for b in range(early):
-        own_block(b)
-
-    @pl.when(me > 0)
-    def _():
-        for copy in to_next(tile):
-            copy.wait_recv()
-
-    @pl.when(me < size - 1)
-    def _():
-        for copy in to_prev(tile):
-            copy.wait_recv()
-
-    for c in range(ncol):
         for ref, src, at in (
             (kx, kp_ref, 0), (vx, vp_ref, 0), (qx, qp_ref, 0),
             (kx, kn_ref, big + length), (vx, vn_ref, big + length), (qx, qn_ref, pad + length),
@@ -308,33 +295,43 @@
         ):
             ref[c, at : at + src.shape[0], :] = src[:, cut(c)].astype(F32)
 
+    def own_block(b):
+        for c in range(ncol):
+            for r in range(span // ROWS):
+                own(b * span + r * ROWS, c, b == nblk - 1)
+
     def rows_of(ref, c, row):
         return ref[c, row : row + ROWS, :]
 
-    for c in range(ncol):
-        make_z(0, c, rows_of(kx, c, big), rows_of(vx, c, big), True, False)
-        make_g(0, c, rows_of(qx, c, pad), rows_of(gx, c, 0), False)
-    for b in range(1, early):
+    def forward_z(b):
         forward(zh, zl, b, zw.at[b + 1])
+
+    def forward_g(b):
         forward(gh, gl, b, gw.at[b])
-    forward(zh, zl, 0, zw.at[1])
-    forward(gh, gl, 0, gw.at[0])
-    for b in range(early, nblk):
+
+    mid = nblk // 2
+    for b in range(nblk):
         own_block(b)
-        forward(zh, zl, b, zw.at[b + 1])
-        forward(gh, gl, b, gw.at[b])
-    for c in range(ncol):
-        for r in range(span // ROWS):
-            row = r * ROWS - span
-            make_z(row, c, rows_of(kx, c, row + big), rows_of(vx, c, row + big), False, False)
-    forward(zh, zl, -1, zw.at[0])
+        if b >= mid - 1:
+            forward_z(b)
+        if b >= mid:
+            forward_g(b)
     for c in range(ncol):
         for r in range(span // ROWS + 1):
             row = length + r * ROWS
             make_g(row, c, rows_of(qx, c, row + pad), rows_of(gx, c, row), True, r < span // ROWS)
         row = length
         make_z(row, c, rows_of(kx, c, row + big), rows_of(vx, c, row + big), True, True, False)
-    forward(gh, gl, nblk, gw.at[nblk])
+    forward_g(nblk)
+    for c in range(ncol):
+        for r in range(span // ROWS):
+            row = r * ROWS - span
+            make_z(row, c, rows_of(kx, c, row + big), rows_of(vx, c, row + big), False, False)
+    for b in range(mid - 1, -2, -1):
+        if b < mid - 1:
+            forward_z(b)
+        if b >= 0:
+            forward_g(b)
     back_h = jnp.dot(flip_ref[...], jnp.concatenate(split(taps_h), 0), preferred_element_type=F32)
     line = lax.broadcasted_iota(jnp.int32, (8, lane), 0)
     for c in range(ncol):
@@ -402,14 +399,9 @@
             acc[im, col] = ai
         return 0
 
-    @pl.when(tile > 0)
-    def _():
-        join_long(tile - 1)
-        join_small(tile - 1)
-
     late = range(nblk // 2, nblk)
-    lax.fori_loop(0, steps // 2, functools.partial(product, late, 1), 0, unroll=UNROLL)
-    lax.fori_loop(steps // 2, steps, functools.partial(product, late, -1), 0, unroll=UNROLL)
+    for n in range(steps):
+        product(late, 1 if n < steps // 2 else -1, n, 0)
 
     def inverse(at, out):
         both = jnp.dot(ih_ref[...], wide(prod[at, 0, c] for c in range(ncol)), preferred_element_type=F32)
@@ -476,8 +468,9 @@
 
     @pl.when(tile == tiles - 1)
     def _():
-        join_long(tiles - 1)
-        join_small(tiles - 1)
+        for t in range(max(tiles - 2, 0), tiles):
+            join_long(t)
+            join_small(t)
 
         def finish(t, _):
             cols = cols_of(t)
@@ -585,7 +578,7 @@
             *[pltpu.VMEM(m.shape, BF16) for m in mats],
             strips(length + big + pad), strips(length + big + pad), strips(length + big + pad), strips(length + big),
             strips(length + pad), strips(length + pad), strips(span + pad), strips(span + pad),
-            *[halves(4, ncol, span) for _ in range(4)],
+            *[halves(nblk + 1, ncol, span) for _ in range(4)],
             cells(nblk + 1, 2 * span), cells(nblk + 1, 2 * span), cells(2 * span), cells(2, span), cells(2, span),
             halves(2 * nblk + 1, 2, ncol, 2 * span), cells(2 * span), cells(span),
             strips(length + pad), strips(length + pad), strips(length + pad), cells(3, ntap, 8),

time: 51.7 us -> 48.1 us (0.930)
  Pallas kernels: 50.9 us -> 47.3 us
    pallas_call x1, Pallas kernels: 47.7 us -> 44.2 us  [body(): pl.pallas_call(functools.partial(kernel, size, length, span, ntap, pad),...]
where the time goes in v2:
time: 48.1 us; the launch traced here: 47.9 us
  Pallas kernels  47.3 us (98%)
  between operations  0.64 us (1%)
    pallas_call x1, Pallas kernels, body(): pl.pallas_call(functools.partial(kernel, size, length, span, ntap, pad),...  44.2 us
    pallas_call x1, Pallas kernels, body(): pl.pallas_call(settle, out_shape=tuple((jax.ShapeDtypeStruct((length, cha...  3.13 us

profile of v2, /device:TPU:0, one launch (start us, length us, event | category | flops | bytes accessed | tf_op | source)
XLA Modules:
  0.0 47.9 jit_solution(8800436756949156217)
XLA Ops:
  0.6 44.2 %hyena_back.1 = (bf16[16,512,128]{2,1,0:T(8,128)(2,1)S(1)}, bf16[16,512,128]{2,1,0:T(8,128)(2,1)S(1)}, bf16[16,512,128]{2,1,0:T(8,128)(2,1)S(1)}, f32[16,2048]{1...) custom-call(bf16[512,2048]{1,0:T(8,128)(2,1)} %q_all.1, bf16[512,2048]{1,0:T(8,128)(2,1)} %k_all.1, ...), custom_call_target="tpu_custom_call" | custom-call | tf_op jit(solution)/shard_map/hyena_back/pallas_call | solution.py:564
  44.8 3.1 %settle.1 = (bf16[512,2048]{1,0:T(8,128)(2,1)}, bf16[512,2048]{1,0:T(8,128)(2,1)}, bf16[512,2048]{1,0:T(8,128)(2,1)}, f32[16,2048]{1,0:T(8,128)}, f32[3,3,2048]{2,1,0:T(4,128)}, /*index=5*/f32[1,2048]{1,0:T(1,128)}) custom-call(bf16[16,512,128]{2,1,0:T(8,128)(2,1)S(1)} %get-tuple-element.18.refs_0_, bf16[16,512,128]{2,1,0:T(8,128)(2,1)S(1)} %get-tuple-element.19.refs_1_, ...), custom_call_target="tpu_custom_call" | custom-call | tf_op jit(solution)/shard_map/settle/pallas_call | solution.py:603

commit v3 on v2

--- a/solution.py
+++ b/solution.py
@@ -199,9 +199,12 @@
     for copy in loads(tile):
         copy.wait()
 
+    @pl.when(tile > 0)
+    def _():
+        join_long(tile - 1)
+
     @pl.when(tile > 1)
     def _():
-        join_long(tile - 2)
         join_small(tile - 2)
 
     @pl.when(me > 0)
@@ -468,8 +471,8 @@
 
     @pl.when(tile == tiles - 1)
     def _():
+        join_long(tiles - 1)
         for t in range(max(tiles - 2, 0), tiles):
-            join_long(t)
             join_small(t)
 
         def finish(t, _):

time: 48.1 us -> 47.9 us (level)
  no operation moved by 1% of the time
where the time goes in v3:
time: 47.9 us; the launch traced here: 47.7 us
  Pallas kernels  47.1 us (98%)
  between operations  0.64 us (1%)
    pallas_call x1, Pallas kernels, body(): pl.pallas_call(functools.partial(kernel, size, length, span, ntap, pad),...  43.9 us
    pallas_call x1, Pallas kernels, body(): pl.pallas_call(settle, out_shape=tuple((jax.ShapeDtypeStruct((length, cha...  3.13 us

profile of v3, /device:TPU:0, one launch (start us, length us, event | category | flops | bytes accessed | tf_op | source)
XLA Modules:
  0.0 47.7 jit_solution(4120586180240474687)
XLA Ops:
  0.6 43.9 %hyena_back.1 = (bf16[16,512,128]{2,1,0:T(8,128)(2,1)S(1)}, bf16[16,512,128]{2,1,0:T(8,128)(2,1)S(1)}, bf16[16,512,128]{2,1,0:T(8,128)(2,1)S(1)}, f32[16,2048]{1...) custom-call(bf16[512,2048]{1,0:T(8,128)(2,1)} %q_all.1, bf16[512,2048]{1,0:T(8,128)(2,1)} %k_all.1, ...), custom_call_target="tpu_custom_call" | custom-call | tf_op jit(solution)/shard_map/hyena_back/pallas_call | solution.py:567
  44.6 3.1 %settle.1 = (bf16[512,2048]{1,0:T(8,128)(2,1)}, bf16[512,2048]{1,0:T(8,128)(2,1)}, bf16[512,2048]{1,0:T(8,128)(2,1)}, f32[16,2048]{1,0:T(8,128)}, f32[3,3,2048]{2,1,0:T(4,128)}, /*index=5*/f32[1,2048]{1,0:T(1,128)}) custom-call(bf16[16,512,128]{2,1,0:T(8,128)(2,1)S(1)} %get-tuple-element.18.refs_0_, bf16[16,512,128]{2,1,0:T(8,128)(2,1)S(1)} %get-tuple-element.19.refs_1_, ...), custom_call_target="tpu_custom_call" | custom-call | tf_op jit(solution)/shard_map/settle/pallas_call | solution.py:606
